TPU v7x, 32 devices: a whole 2x2x4 slice. The times are simulated.
32 devices in a mesh: ta: 4 (over z), gz: 2 (over x), xy: 4 (over y, core).
Axes of the slice: x: 2, y: 2, z: 4, core: 2. Of those that a mesh axis runs over, the one named last changes fastest.
Arguments:
- links: float32 [4, 2, 4, 4, 9, 4608], P('ta', 'gz', 'xy'), may hold values from -1 to 3
- eigvecs: float32 [4, 2, 4, 4, 48, 128], P('ta', 'gz', 'xy'), may hold values from -1 to 1
- eig_real: float32 [64], replicated, may hold values from 0.8 to 2.5
- eig_imag: float32 [64], replicated, may hold values from -0.5 to 0.5
- rhs: float32 [4, 2, 4, 4, 48, 128], P('ta', 'gz', 'xy'), may hold values from -3000 to 3000
Outputs:
- solution: float32 [4, 2, 4, 4, 48, 128], P('ta', 'gz', 'xy')
- residual: float32 [4, 2, 4, 4, 48, 128], P('ta', 'gz', 'xy')
All inputs are finite; a program needn't handle non-finite values.
Results may differ from a plain program's by a relative error of at most 0.0003.
Values sent between devices are 32-bit elements; how exact they have to be, the bound alone decides.
A program may use at most 64 MiB of HBM per device.

v0:
```python
import functools

import jax
import jax.numpy as jnp
from jax import lax
from jax.experimental import pallas as pl
from jax.experimental.pallas import tpu as pltpu
from jax.sharding import PartitionSpec as P

SWEEPS = 4
DIRECT = 32
HIGH = lax.Precision.HIGHEST
MESH = pl.DeviceIdType.MESH
F32, BF16 = jnp.float32, jnp.bfloat16


def split(x):
    first = x.astype(BF16)
    x = x - first.astype(F32)
    second = x.astype(BF16)
    return first, second, (x - second.astype(F32)).astype(BF16)


def kernel(
    sizes, dims, links_hbm, v_ref, er_ref, ei_ref, rhs_ref, sol_ref, res_ref,
    links, flat, mats, srcs, acc, fields, halos, w_ref, cfull, cpart, rs_buf, ct_buf,
    ag_buf, at_buf, ap_buf, vw,
    link_sem, halo_send, halo_recv, rs_send, rs_recv, ct_send, ct_recv, ag_send, ag_recv,
    at_send, at_recv, ap_send, ap_recv,
):
    nt, nz, nx = sizes
    ny, dof, lanes = dims
    half = lanes // 2
    plane = nz * nx
    it, iz, ix = lax.axis_index("ta"), lax.axis_index("gz"), lax.axis_index("xy")
    me = iz * nx + ix

    link_copy = pltpu.make_async_copy(links_hbm, links, link_sem)
    link_copy.start()

    def plane_peer(k):
        p = lax.rem(me + k, plane)
        return p, {"ta": it, "gz": lax.div(p, nx), "xy": lax.rem(p, nx)}

    def time_peer(k):
        p = lax.rem(it + k, nt)
        return p, {"ta": p, "gz": iz, "xy": ix}

    everyone = nt * plane
    rank = it * plane + me

    def any_peer(k):
        p = lax.rem(rank + k, everyone)
        r = lax.rem(p, plane)
        return p, {"ta": lax.div(p, plane), "gz": lax.div(r, nx), "xy": lax.rem(r, nx)}

    direct = everyone <= DIRECT
    if direct:
        greeted = [any_peer(k)[1] for k in range(1, everyone)]
    else:
        greeted = [plane_peer(k)[1] for k in range(1, plane)]
        greeted += [time_peer(k)[1] for k in range(1, nt)]
    barrier = pltpu.get_barrier_semaphore()
    for target in greeted:
        pl.semaphore_signal(barrier, inc=1, device_id=target, device_id_type=MESH)

    def neighbours(axis, index, n):
        base = {"ta": it, "gz": iz, "xy": ix}
        up, down = dict(base), dict(base)
        up[axis] = lax.rem(index + 1, n)
        down[axis] = lax.rem(index + n - 1, n)
        return up, down

    outgoing, groups, slot = [], {}, 0
    for axis, index, n, d in (("ta", it, nt, 1), ("xy", ix, nx, 3), ("gz", iz, nz, 2)):
        up, down = neighbours(axis, index, n)
        if n == 2:
            outgoing.append((axis, slot, up))
            groups[axis] = [(slot, (d, d + 4))]
            slot += 1
        else:
            turn = jnp.where(index == n - 1, 1, 0)
            for t in (turn, 1 - turn):
                target = dict(up)
                target[axis] = lax.rem(index + n - 1 + 2 * t, n)
                outgoing.append((axis, slot + t, target))
            groups[axis] = [(slot, (d,)), (slot + 1, (d + 4,))]
            slot += 2
    far, near = groups["ta"], groups["xy"] + groups["gz"]

    def send_field(rnd, src, axes=("ta", "xy", "gz")):
        out = []
        for axis, s, target in outgoing:
            if axis not in axes:
                continue
            c = pltpu.make_async_remote_copy(
                src_ref=src, dst_ref=halos.at[rnd, s],
                send_sem=halo_send.at[rnd, s], recv_sem=halo_recv.at[rnd, s],
                device_id=target, device_id_type=MESH,
            )
            c.start()
            out.append(c)
        return out

    def arrived(rnd, s):
        pltpu.make_async_remote_copy(
            src_ref=v_ref, dst_ref=halos.at[rnd, s],
            send_sem=halo_send.at[rnd, s], recv_sem=halo_recv.at[rnd, s],
            device_id=outgoing[0][2], device_id_type=MESH,
        ).wait_recv()

    def share(buf, mine, n, peer, send, recv):
        out = []
        for k in range(1, n):
            c = pltpu.make_async_remote_copy(
                src_ref=buf.at[mine], dst_ref=buf.at[mine],
                send_sem=send.at[k], recv_sem=recv.at[k],
                device_id=peer(k)[1], device_id_type=MESH,
            )
            c.start()
            out.append(c)
        return out

    def recv_all(copies):
        for c in copies:
            c.wait_recv()

    def add_slots(buf, n):
        parts = [buf[p] for p in range(n)]
        while len(parts) > 1:
            odd = parts[len(parts) // 2 * 2 :]
            parts = [a + b for a, b in zip(parts[::2], parts[1::2])] + odd
        return parts[0]

    lane = lax.broadcasted_iota(jnp.int32, (1, lanes), 1)
    low = lane < half
    jsign = jnp.where(low, -1.0, 1.0).astype(F32)

    def swap(x):
        return pltpu.roll(x, half, 1)

    sends = []
    rows = v_ref[...].reshape(ny * dof, lanes)
    cross = lax.dot_general(
        rows, rhs_ref[...].reshape(ny * dof, lanes), (((0,), (0,)), ((), ())),
        precision=HIGH, preferred_element_type=F32,
    )
    cfull[...] = cross[:half] - jsign * swap(cross[half:])
    part = half // plane
    for p in range(plane):
        cpart[p] = cfull[p * part : (p + 1) * part]
    pl.semaphore_wait(barrier, len(greeted))
    rs_copies = []
    for k in range(1, plane):
        p, target = plane_peer(k)
        c = pltpu.make_async_remote_copy(
            src_ref=cpart.at[p], dst_ref=rs_buf.at[me],
            send_sem=rs_send.at[k], recv_sem=rs_recv.at[k],
            device_id=target, device_id_type=MESH,
        )
        c.start()
        rs_copies.append(c)
    rs_buf[me] = cpart[me]
    sends += rs_copies
    sends += send_field(0, v_ref, ("xy", "gz"))

    link_copy.wait()
    two = 2 * dof
    valid = lane < two

    def pick(pair, b, j):
        at = j * two
        base, off = (at // 128) * 128, at % 128
        start = pl.multiple_of(b * (4 * two), 128) + base
        width = 128 if off + two <= 128 else 256
        x = [links[d, :, pl.ds(start, width)] for d in pair]
        x = jnp.concatenate(x, 0) if len(x) > 1 else x[0]
        if off:
            x = pltpu.roll(x, width - off, 1)
        return jnp.where(valid, x[:, :128], 0.0)

    def relayout(b, carry):
        for pair in ((0, 1), (2, 3), (4, 5), (6, 7), (8,)):
            for j in range(4):
                row = pair[0] * ny * dof + 4 * b + j
                flat[pl.ds(row, len(pair) * ny, stride=dof), :] = pick(pair, b, j)
        return carry

    lax.fori_loop(0, dof // 4, relayout, 0)

    def direction(y, d):
        return flat[pl.ds((d * ny + y) * dof, dof), :]

    order = [(0,), (4,), (8,)] + [ds for _, ds in near] + [ds for _, ds in far]
    for y in range(ny):
        for m, ds in enumerate(order):
            x = direction(y, ds[0])
            for d in ds[1:]:
                x = x + direction(y, d)
            if ds[0]:
                x = -x
            for i, piece in enumerate(split(x)):
                mats[y, i * dof : (i + 1) * dof, m * 128 : (m + 1) * 128] = piece
    srcs[:, :, two:, :] = jnp.zeros((srcs.shape[0], ny, srcs.shape[2] - two, 3 * lanes), BF16)

    def prepare(m, y, x):
        for i, piece in enumerate(split(x)):
            srcs[m, y, :dof, i * lanes : (i + 1) * lanes] = piece
        for i, piece in enumerate(split(swap(x) * jsign)):
            srcs[m, y, dof:two, i * lanes : (i + 1) * lanes] = piece

    def product(y, m0, blocks):
        right = jnp.concatenate([srcs[s, z] for s, z in blocks], 0)
        left = mats[y, :, m0 * 128 : (m0 + len(blocks)) * 128]
        main = jnp.dot(left, right[:, : 2 * lanes], preferred_element_type=F32)
        small = jnp.dot(left[:dof], right[:, 2 * lanes :], preferred_element_type=F32)
        second = main[dof : 2 * dof]
        small = small + main[2 * dof :, :lanes] + second[:, lanes:]
        return main[:dof, :lanes] + (main[:dof, lanes:] + second[:, :lanes] + small)

    def begin(field):
        for y in range(ny):
            prepare(0, y, field[y])
        for y in range(ny):
            acc[y] = product(y, 0, [(0, y), (0, (y + 1) % ny), (0, (y - 1) % ny)])

    def middle(rnd):
        for i, (s, _) in enumerate(near):
            arrived(rnd, s)
            for y in range(ny):
                prepare(1 + i, y, halos[rnd, s, y])
        for y in range(ny):
            acc[y] += product(y, 3, [(1 + i, y) for i in range(len(near))])

    def finish(rnd, emit):
        first = 1 + len(near)
        for i, (s, _) in enumerate(far):
            arrived(rnd, s)
            for y in range(ny):
                prepare(first + i, y, halos[rnd, s, y])
        for y in range(ny):
            t = acc[y] + product(y, 3 + len(near), [(first + i, y) for i in range(len(far))])
            emit(y, t)

    recv_all(rs_copies)
    total = rs_buf[0]
    for p in range(1, plane):
        total = total + rs_buf[p]
    ct_buf[it] = total
    ct_copies = share(ct_buf, it, nt, time_peer, ct_send, ct_recv)
    sends += ct_copies
    sends += send_field(0, v_ref, ("ta",))

    begin(v_ref)

    recv_all(ct_copies)
    total = ct_buf[0]
    for p in range(1, nt):
        total = total + ct_buf[p]
    ag_buf[me] = total
    ag_copies = share(ag_buf, me, plane, plane_peer, ag_send, ag_recv)
    sends += ag_copies

    middle(0)

    def keep(y, value):
        w_ref[y] = value

    finish(0, keep)
    for i, ref in enumerate((v_ref, w_ref)):
        one, other, third = split(ref[...].reshape(ny * dof, lanes))
        for j, piece in enumerate((one, other, one, third)):
            vw[i * ny * dof : (i + 1) * ny * dof, j * lanes : (j + 1) * lanes] = piece

    recv_all(ag_copies)
    for p in range(plane):
        cfull[p * part : (p + 1) * part] = ag_buf[p]
    corr = cfull[...]
    eye = lax.broadcasted_iota(jnp.int32, (half, half), 0) == lax.broadcasted_iota(
        jnp.int32, (half, half), 1
    )
    er = jnp.sum(jnp.where(eye, er_ref[...], 0.0), axis=1, keepdims=True)
    ei = jnp.sum(jnp.where(eye, ei_ref[...], 0.0), axis=1, keepdims=True)
    coef = (corr * er - jsign * swap(corr) * ei) / (er * er + ei * ei)
    b1, b2, b3 = split(jnp.concatenate([coef, jsign * swap(coef)], 0))
    block = jnp.concatenate([b1, b2], 1)
    block = jnp.concatenate([block, block], 0)
    both = jnp.dot(vw[:, : 2 * lanes], block, preferred_element_type=F32)
    small = jnp.dot(
        vw[:, 2 * lanes :], jnp.concatenate([b3, b1], 0), preferred_element_type=F32
    )
    both = both[:, :lanes] + (both[:, lanes:] + small)
    n = ny * dof
    r0 = rhs_ref[...] - both[n:].reshape(ny, dof, lanes)
    fields[0] = r0
    sends += send_field(1, fields.at[0])
    sol_ref[...] = both[:n].reshape(ny, dof, lanes)
    res_ref[...] = r0

    begin(fields.at[0])
    middle(1)

    def to_first(y, value):
        fields[1, y] = value

    finish(1, to_first)

    for sweep in range(SWEEPS):
        image = fields.at[sweep + 1]
        last = sweep + 1 == SWEEPS
        s1 = jnp.zeros((1, lanes), F32)
        s2, s3 = s1, s1
        for y in range(ny):
            f, r = image[y], res_ref[y]
            s1 = s1 + jnp.sum(f * r, axis=0, keepdims=True)
            s2 = s2 + jnp.sum(f * swap(r), axis=0, keepdims=True)
            s3 = s3 + jnp.sum(f * f, axis=0, keepdims=True)
        num = jnp.where(low, s1 + swap(s1), swap(s2) - s2)
        den = s3 + swap(s3)
        row = lax.broadcasted_iota(jnp.int32, (2, lanes), 0)
        tbuf, pbuf = at_buf.at[sweep], ap_buf.at[sweep]
        mine, n, peer = (rank, everyone, any_peer) if direct else (it, nt, time_peer)
        tbuf[mine] = jnp.where(row == 0, num, den)
        t_copies = share(tbuf, mine, n, peer, at_send.at[sweep], at_recv.at[sweep])
        sends += t_copies
        if not last:
            sends += send_field(sweep + 2, image)
            begin(image)
        if direct and not last:
            middle(sweep + 2)
        recv_all(t_copies)
        total = add_slots(tbuf, n)
        if not direct:
            pbuf[me] = total
            p_copies = share(pbuf, me, plane, plane_peer, ap_send.at[sweep], ap_recv.at[sweep])
            sends += p_copies
            if not last:
                middle(sweep + 2)
            recv_all(p_copies)
            total = add_slots(pbuf, plane)
        a = total[0:1] / total[1:2]
        sa = swap(a)
        ar = jnp.where(low, a, sa)
        ai = jnp.where(low, sa, a) * jsign
        for y in range(ny):
            f, r = image[y], res_ref[y]
            sol_ref[y] = sol_ref[y] + (ar * r + ai * swap(r))
            res_ref[y] = r - (ar * f + ai * swap(f))
        if not last:

            def update(y, value):
                fields[sweep + 2, y] = image[y] - (ar * value + ai * swap(value))

            finish(sweep + 2, update)
    for c in sends:
        c.wait_send()


def hand_over(a_ref, b_ref, sol_ref, res_ref):
    sol_ref[...] = a_ref[...]
    res_ref[...] = b_ref[...]


def local(sizes, links, eigvecs, eig_real, eig_imag, rhs):
    nt, nz, nx = sizes
    plane = nz * nx
    ny, dof, lanes = rhs.shape[3:]
    half = lanes // 2
    field = (ny, dof, lanes)
    ndir = links.shape[4]
    slots = sum(1 if n == 2 else 2 for n in sizes)
    part = half // plane
    rounds = SWEEPS + 1
    first = nt * plane if nt * plane <= DIRECT else nt
    vmem, dma = pltpu.VMEM, pltpu.SemaphoreType.DMA
    spec = pl.BlockSpec(memory_space=pltpu.VMEM)
    sol, res = pl.pallas_call(
        functools.partial(kernel, sizes, field),
        out_shape=[jax.ShapeDtypeStruct(field, F32)] * 2,
        in_specs=[pl.BlockSpec(memory_space=pl.ANY)] + [spec] * 4,
        out_specs=[spec] * 2,
        scratch_shapes=[
            vmem((ndir, ny, links.shape[5]), F32),
            vmem((ndir * ny * dof, 128), F32),
            vmem((ny, 3 * dof, (3 + slots) * 128), BF16),
            vmem((1 + slots, ny, 128, 3 * lanes), BF16),
            vmem(field, F32),
            vmem((rounds,) + field, F32),
            vmem((rounds, slots) + field, F32),
            vmem(field, F32),
            vmem((half, lanes), F32),
            vmem((plane, part, lanes), F32),
            vmem((plane, part, lanes), F32),
            vmem((nt, part, lanes), F32),
            vmem((plane, part, lanes), F32),
            vmem((SWEEPS, first, 2, lanes), F32),
            vmem((SWEEPS, plane, 2, lanes), F32),
            vmem((2 * ny * dof, 4 * lanes), BF16),
            dma,
            dma((rounds, slots)),
            dma((rounds, slots)),
            dma((plane,)),
            dma((plane,)),
            dma((nt,)),
            dma((nt,)),
            dma((plane,)),
            dma((plane,)),
            dma((SWEEPS, first)),
            dma((SWEEPS, first)),
            dma((SWEEPS, plane)),
            dma((SWEEPS, plane)),
        ],
        compiler_params=pltpu.CompilerParams(collective_id=0, has_side_effects=True),
    )(
        links.reshape(links.shape[3:]).transpose(1, 0, 2),
        eigvecs.reshape(field),
        eig_real.reshape(1, -1),
        eig_imag.reshape(1, -1),
        rhs.reshape(field),
    )
    sol, res = pl.pallas_call(
        hand_over,
        out_shape=[jax.ShapeDtypeStruct(field, F32)] * 2,
        in_specs=[spec] * 2,
        out_specs=[spec] * 2,
    )(sol, res)
    return (sol.reshape(rhs.shape), res.reshape(rhs.shape))


def solution(mesh):
    whole = P("ta", "gz", "xy", None, None, None)
    sizes = tuple(mesh.shape[a] for a in ("ta", "gz", "xy"))
    return jax.shard_map(
        functools.partial(local, sizes),
        mesh=mesh,
        in_specs=(whole, whole, P(), P(), whole),
        out_specs=(whole, whole),
        check_vma=False,
    )
```

profile of v0, /device:TPU:0, one launch (start us, length us, event | category | flops | bytes accessed | tf_op | source)
XLA Modules:
  0.0 57.3 jit_solution(7744305886457963179)
XLA Ops:
  0.6 55.0 %shard_map.68 = (f32[4,48,128]{2,1,0:T(8,128)}, f32[4,48,128]{2,1,0:T(8,128)}) custom-call(f32[9,4,4608]{2,1,0:T(4,128)} %bitcast.9, f32[4,48,128]{2,1,0:T(8,128)} %bitcast.10, f32[1,64]{1,0:T(1,128)} %bitcast.12, f32[1,64]{1,0:T(1,128)} %bitcast.13, f32[4,48,128]{2,1,0:T(8,128)} %bitcast.11), custom_call_target="tpu_custom_call" | custom-call | tf_op jit(solution)/shard_map/pallas_call | solution.py:377
  55.7 1.6 %shard_map.69 = (f32[4,48,128]{2,1,0:T(8,128)}, f32[4,48,128]{2,1,0:T(8,128)}) custom-call(f32[4,48,128]{2,1,0:T(8,128)} %get-tuple-element.6.a_ref, f32[4,48,128]{2,1,0:T(8,128)} %get-tuple-element.7.b_ref), custom_call_target="tpu_custom_call" | custom-call | tf_op jit(solution)/shard_map/pallas_call | solution.py:421
where the time goes:
time: 57.5 us; the launch traced here: 57.3 us
  Pallas kernels  56.6 us (98%)
  between operations  0.64 us (1%)
    pallas_call x1, Pallas kernels, local(): pl.pallas_call(functools.partial(kernel, sizes, field), out_shape=[jax.Sh...  55 us
    pallas_call x1, Pallas kernels, local(): pl.pallas_call(hand_over, out_shape=[jax.ShapeDtypeStruct(field, F32)] *...  1.62 us

commit v1 on v0

v1 whole, which is shorter than its diff:
```python
import functools

import jax
import jax.numpy as jnp
from jax import lax
from jax.experimental import pallas as pl
from jax.experimental.pallas import tpu as pltpu
from jax.sharding import PartitionSpec as P

SWEEPS = 4
DIRECT = 32
MESH = pl.DeviceIdType.MESH
F32, BF16 = jnp.float32, jnp.bfloat16


def split(x):
    first = x.astype(BF16)
    return first, (x - first.astype(F32)).astype(BF16)


def pair(x):
    return jnp.concatenate(split(x), 1)


def pad_to(n, m):
    return -(-n // m) * m


def kernel(
    sizes, dims, links_hbm, v_hbm, er_hbm, ei_hbm, rhs_hbm, sol_ref, res_ref,
    links, v_ref, rhs_ref, er_ref, ei_ref, flat, mats, acc, pcs, fields, halos, vw, start_ref,
    g_ref, cpart, rs_buf, ct_buf, ag_buf, ec, st_buf, sp_buf, sd_buf,
    in_sem, halo_send, halo_recv, rs_send, rs_recv, ct_send, ct_recv, ag_send, ag_recv,
    st_send, st_recv, sp_send, sp_recv, sd_send, sd_recv,
):
    nt, nz, nx = sizes
    ny, dof, lanes = dims
    half = lanes // 2
    plane = nz * nx
    it, iz, ix = lax.axis_index("ta"), lax.axis_index("gz"), lax.axis_index("xy")
    me = iz * nx + ix
    part = half // plane

    loads = []
    for i, (src, dst) in enumerate(
        ((v_hbm, v_ref), (rhs_hbm, rhs_ref), (links_hbm, links), (er_hbm, er_ref), (ei_hbm, ei_ref))
    ):
        c = pltpu.make_async_copy(src, dst, in_sem.at[i])
        c.start()
        loads.append(c)

    def plane_peer(k):
        p = lax.rem(me + k, plane)
        return p, {"ta": it, "gz": lax.div(p, nx), "xy": lax.rem(p, nx)}

    def time_peer(k):
        p = lax.rem(it + k, nt)
        return p, {"ta": p, "gz": iz, "xy": ix}

    everyone = nt * plane
    rank = it * plane + me

    def any_peer(k):
        p = lax.rem(rank + k, everyone)
        r = lax.rem(p, plane)
        return p, {"ta": lax.div(p, plane), "gz": lax.div(r, nx), "xy": lax.rem(r, nx)}

    direct = everyone <= DIRECT
    greeted = [plane_peer(k)[1] for k in range(1, plane)]
    greeted += [time_peer(k)[1] for k in range(1, nt)]
    barrier = pltpu.get_barrier_semaphore()
    for target in greeted:
        pl.semaphore_signal(barrier, inc=1, device_id=target, device_id_type=MESH)

    def neighbours(axis, index, n):
        base = {"ta": it, "gz": iz, "xy": ix}
        up, down = dict(base), dict(base)
        up[axis] = lax.rem(index + 1, n)
        down[axis] = lax.rem(index + n - 1, n)
        return up, down

    outgoing, groups, slot = [], {}, 0
    for axis, index, n, d in (("ta", it, nt, 1), ("xy", ix, nx, 3), ("gz", iz, nz, 2)):
        up, down = neighbours(axis, index, n)
        if n == 2:
            outgoing.append((axis, slot, up))
            groups[axis] = [(slot, (d, d + 4))]
            slot += 1
        else:
            turn = jnp.where(index == n - 1, 1, 0)
            for t in (turn, 1 - turn):
                target = dict(up)
                target[axis] = lax.rem(index + n - 1 + 2 * t, n)
                outgoing.append((axis, slot + t, target))
            groups[axis] = [(slot, (d,)), (slot + 1, (d + 4,))]
            slot += 2
    far, near = groups["ta"], groups["xy"] + groups["gz"]
    sends = []

    def send_chunk(rnd, src, y, axes=("ta", "xy", "gz")):
        for axis, s, target in outgoing:
            if axis not in axes:
                continue
            c = pltpu.make_async_remote_copy(
                src_ref=src.at[y], dst_ref=halos.at[rnd, s, y],
                send_sem=halo_send.at[rnd, s, y], recv_sem=halo_recv.at[rnd, s, y],
                device_id=target, device_id_type=MESH,
            )
            c.start()
            sends.append(c)

    def arrived(rnd, s, y):
        pltpu.make_async_remote_copy(
            src_ref=v_ref.at[y], dst_ref=halos.at[rnd, s, y],
            send_sem=halo_send.at[rnd, s, y], recv_sem=halo_recv.at[rnd, s, y],
            device_id=outgoing[0][2], device_id_type=MESH,
        ).wait_recv()

    def share(buf, mine, n, peer, send, recv):
        out = []
        for k in range(1, n):
            c = pltpu.make_async_remote_copy(
                src_ref=buf.at[mine], dst_ref=buf.at[mine],
                send_sem=send.at[k], recv_sem=recv.at[k],
                device_id=peer(k)[1], device_id_type=MESH,
            )
            c.start()
            out.append(c)
        sends.extend(out)
        return out

    def recv_all(copies):
        for c in copies:
            c.wait_recv()

    def add_slots(buf, n):
        parts = [buf[p] for p in range(n)]
        while len(parts) > 1:
            odd = parts[len(parts) // 2 * 2 :]
            parts = [a + b for a, b in zip(parts[::2], parts[1::2])] + odd
        return parts[0]

    lane = lax.broadcasted_iota(jnp.int32, (1, lanes), 1)
    low = lane < half
    jsign = jnp.where(low, -1.0, 1.0).astype(F32)

    def swap(x):
        return pltpu.roll(x, half, 1)

    def real(c):
        return jnp.where(low, c, swap(c))

    def imag(c):
        return jnp.where(low, swap(c), c)

    def factor(c):
        return real(c), imag(c) * jsign

    def times(f, x):
        return f[0] * x + f[1] * swap(x)

    def mul(a, b):
        return times(factor(a), b)

    def conj(a):
        return -jsign * a

    one = jnp.where(low, 1.0, 0.0).astype(F32)

    loads[0].wait()
    loads[1].wait()
    rows = pair(v_ref[...].reshape(ny * dof, lanes))
    cross = lax.dot_general(
        rows, pair(rhs_ref[...].reshape(ny * dof, lanes)), (((0,), (0,)), ((), ())),
        preferred_element_type=F32,
    )
    cross = cross[:lanes, :lanes] + (cross[:lanes, lanes:] + cross[lanes:, :lanes])
    corr = cross[:half] - jsign * swap(cross[half:])
    for p in range(plane):
        cpart[p] = corr[p * part : (p + 1) * part]
    pl.semaphore_wait(barrier, len(greeted))
    rs_copies = []
    for k in range(1, plane):
        p, target = plane_peer(k)
        c = pltpu.make_async_remote_copy(
            src_ref=cpart.at[p], dst_ref=rs_buf.at[me],
            send_sem=rs_send.at[k], recv_sem=rs_recv.at[k],
            device_id=target, device_id_type=MESH,
        )
        c.start()
        rs_copies.append(c)
    rs_buf[me] = cpart[me]
    sends += rs_copies
    for y in range(ny):
        send_chunk(0, v_ref, y, ("xy", "gz"))

    loads[3].wait()
    loads[4].wait()
    theta = half / jnp.sum(er_ref[...], axis=1, keepdims=True)
    eye = lax.broadcasted_iota(jnp.int32, (half, half), 0) == lax.broadcasted_iota(
        jnp.int32, (half, half), 1
    )
    er = jnp.sum(jnp.where(eye, er_ref[...], 0.0), axis=1, keepdims=True)
    ei = jnp.sum(jnp.where(eye, ei_ref[...], 0.0), axis=1, keepdims=True)
    scale = 1.0 / (er * er + ei * ei)
    ec[0] = er * scale + jnp.zeros((half, lanes), F32)
    ec[1] = -jsign * (ei * scale)

    loads[2].wait()
    two = 2 * dof
    valid = lane < two

    def pick(ds, b, j):
        at = j * two
        base, off = (at // 128) * 128, at % 128
        start = pl.multiple_of(b * (4 * two), 128) + base
        width = 128 if off + two <= 128 else 256
        x = [links[d, :, pl.ds(start, width)] for d in ds]
        x = jnp.concatenate(x, 0) if len(x) > 1 else x[0]
        if off:
            x = pltpu.roll(x, width - off, 1)
        return jnp.where(valid, x[:, :128], 0.0)

    def relayout(b, carry):
        for ds in ((0, 1), (2, 3), (4, 5), (6, 7), (8,)):
            for j in range(4):
                row = ds[0] * ny * dof + 4 * b + j
                flat[pl.ds(row, len(ds) * ny, stride=dof), :] = pick(ds, b, j)
        return carry

    lax.fori_loop(0, dof // 4, relayout, 0)

    def direction(y, d):
        return flat[pl.ds((d * ny + y) * dof, dof), :]

    local_group = [(0,), (4,), (8,)]
    near_group = [ds for _, ds in near]
    far_group = [ds for _, ds in far]
    widths = [pad_to(len(g) * dof, 128) for g in (local_group, near_group, far_group)]
    bases = [0, widths[0], widths[0] + widths[1]]
    first_half = lane < dof
    diag = jnp.where(
        lax.broadcasted_iota(jnp.int32, (dof, lanes), 0)
        == lax.broadcasted_iota(jnp.int32, (dof, lanes), 1), 1.0, 0.0,
    )

    def place(parts, width):
        tiles = [jnp.zeros((dof, 128), F32)] * (width // 128)
        for m, p in enumerate(parts):
            t, w = divmod(dof * m, 128)
            r = pltpu.roll(p, w, 1) if w else p
            if w + dof <= 128:
                tiles[t] = tiles[t] + r
            else:
                tiles[t] = tiles[t] + jnp.where(lane >= w, r, 0.0)
                tiles[t + 1] = tiles[t + 1] + jnp.where(lane < w, r, 0.0)
        return jnp.concatenate(tiles, 1)

    def build(y):
        for g, group in enumerate((local_group, near_group, far_group)):
            res, ims = [], []
            for ds in group:
                x = direction(y, ds[0])
                for d in ds[1:]:
                    x = x + direction(y, d)
                x = x * theta
                if not ds[0]:
                    x = diag - x
                res.append(jnp.where(first_half, x, 0.0))
                ims.append(jnp.where(first_half, pltpu.roll(x, 128 - dof, 1), 0.0))
            for h, parts in enumerate((res, ims)):
                for i, piece in enumerate(split(place(parts, widths[g]))):
                    row = (2 * i + h) * dof
                    mats[y, row : row + dof, bases[g] : bases[g] + widths[g]] = piece

    def product(y, g, blocks):
        width = widths[g]
        rest = width - len(blocks) * dof
        if rest:
            blocks = blocks + [jnp.zeros((rest, 2 * lanes), BF16)]
        out = jnp.dot(
            mats[y, :, bases[g] : bases[g] + width], jnp.concatenate(blocks, 0),
            preferred_element_type=F32,
        )
        return out[:two, :lanes] + (out[:two, lanes:] + out[two:, :lanes])

    def begin():
        for y in range(ny):
            acc[y] = product(y, 0, [pcs[y], pcs[(y + 1) % ny], pcs[(y - 1) % ny]])

    def halo_blocks(rnd, y, group):
        blocks = []
        for s, _ in group:
            arrived(rnd, s, y)
            blocks.append(pair(halos[rnd, s, y]))
        return blocks

    def middle(rnd, y):
        acc[y] += product(y, 1, halo_blocks(rnd, y, near))

    def finish(rnd, y):
        t = acc[y] + product(y, 2, halo_blocks(rnd, y, far))
        return t[:dof] + jsign * swap(t[dof:])

    recv_all(rs_copies)
    ct_buf[it] = add_slots(rs_buf, plane)
    ct_copies = share(ct_buf, it, nt, time_peer, ct_send, ct_recv)
    for y in range(ny):
        send_chunk(0, v_ref, y, ("ta",))

    for y in range(ny):
        build(y)
    for y in range(ny):
        pcs[y] = pair(v_ref[y])
    begin()

    recv_all(ct_copies)
    total = add_slots(ct_buf, nt)
    mine = pl.ds(me * part, part)
    ag_buf[me] = total * ec[0, mine] + swap(total) * ec[1, mine]
    ag_copies = share(ag_buf, me, plane, plane_peer, ag_send, ag_recv)

    for y in range(ny):
        middle(0, y)
    inverse = 1.0 / theta
    for y in range(ny):
        v = v_ref[y]
        w = (v - finish(0, y)) * inverse
        for i, piece in enumerate(split(w) + split(v)):
            vw[y, i * dof : (i + 1) * dof] = piece

    recv_all(ag_copies)
    coef = jnp.concatenate([ag_buf[p] for p in range(plane)], 0)
    block = pair(jnp.concatenate([coef, jsign * swap(coef)], 0))

    def expand(y, i):
        out = jnp.dot(vw[y, i * dof : (i + 2) * dof], block, preferred_element_type=F32)
        return out[:dof, :lanes] + (out[:dof, lanes:] + out[dof:, :lanes])

    for y in range(ny):
        r = rhs_ref[y] - expand(y, 0)
        fields[0, y] = r
        send_chunk(1, fields.at[0], y)
        pcs[y] = pair(r)
    for y in range(ny):
        start_ref[y] = expand(y, 2)

    def fold(x):
        return jnp.sum(x.reshape(dof // 8, 8, lanes), axis=0)

    def partials(x0, x1, x2):
        u0, u1 = x0 - x1, x1 - x2
        s0, t0 = swap(x0), swap(u0)
        return [
            fold(p)
            for p in (u0 * x0, u0 * s0, u1 * x0, u1 * s0, u1 * u0, u1 * t0, u0 * u0, u1 * u1)
        ]

    def add(a, b):
        return b if a is None else [p + q for p, q in zip(a, b)]

    def gram(sums):
        s = [jnp.sum(p, axis=0, keepdims=True) for p in sums]
        out = [
            jnp.where(low, s[i] + swap(s[i]), swap(s[i + 1]) - s[i + 1]) for i in (0, 2, 4)
        ]
        out.append(jnp.where(low, s[6] + swap(s[6]), s[7] + swap(s[7])))
        row = lax.broadcasted_iota(jnp.int32, (4, lanes), 0)
        x = out[3]
        for i in (2, 1, 0):
            x = jnp.where(row == i, out[i], x)
        return x

    def steps(total):
        a, b, c, d = (total[i : i + 1] for i in range(4))
        b0 = a / real(d)
        e = mul(conj(b0), c)
        num = mul(conj(b0), b) - mul(real(mul(conj(b0), b0)) * one, c)
        near_one = one - b0
        size0 = real(mul(conj(near_one), near_one))
        size1 = real(mul(conj(b0), b0))
        den = size0 * real(d) + size1 * imag(d) + 2.0 * real(mul(near_one, e))
        b1 = num / den
        both = mul(b0, b1)
        mixed = b0 + b1 - both
        poly = [factor(x) for x in (one - mixed, mixed - both, both)]
        gain = [factor(theta * x) for x in (mixed, both)]
        return poly, gain

    def combine(poly, xs):
        out = times(poly[0], xs[0])
        for p, x in zip(poly[1:], xs[1:]):
            out = out + times(p, x)
        return out

    def step(rnd, y):
        out = finish(rnd, y)
        fields[rnd, y] = out
        if rnd < SWEEPS:
            send_chunk(rnd + 1, fields.at[rnd], y)
            pcs[y] = pair(out)

    LEAD = 2
    poly = gain = None
    sums = None
    for rnd in range(1, SWEEPS + 1):
        begin()
        if rnd == 3:
            for y in range(ny):
                sums = add(sums, partials(fields[0, y], fields[1, y], fields[2, y]))
            st_buf[0, it] = gram(sums)
            early = share(st_buf.at[0], it, nt, time_peer, st_send.at[0], st_recv.at[0])
        if rnd == 4:
            recv_all(early)
            sp_buf[0, me] = add_slots(st_buf.at[0], nt)
            early = share(sp_buf.at[0], me, plane, plane_peer, sp_send.at[0], sp_recv.at[0])
        for y in range(ny + LEAD):
            if y < ny:
                middle(rnd, y)
            if y >= LEAD:
                step(rnd, y - LEAD)
    recv_all(early)
    poly, gain = steps(add_slots(sp_buf.at[0], plane))
    sums = None
    for y in range(ny):
        f = [fields[i, y] for i in range(SWEEPS + 1)]
        g = [combine(poly, f[i : i + 3]) for i in range(3)]
        for i in range(3):
            g_ref[i, y] = g[i]
        start_ref[y] = start_ref[y] + combine(gain, f[:2])
        sums = add(sums, partials(*g))
    if direct:
        sd_buf[rank] = gram(sums)
        last = share(sd_buf, rank, everyone, any_peer, sd_send, sd_recv)
        recv_all(last)
        total = add_slots(sd_buf, everyone)
    else:
        st_buf[1, it] = gram(sums)
        last = share(st_buf.at[1], it, nt, time_peer, st_send.at[1], st_recv.at[1])
        recv_all(last)
        sp_buf[1, me] = add_slots(st_buf.at[1], nt)
        last = share(sp_buf.at[1], me, plane, plane_peer, sp_send.at[1], sp_recv.at[1])
        recv_all(last)
        total = add_slots(sp_buf.at[1], plane)
    poly, gain = steps(total)
    for y in range(ny):
        g = [g_ref[i, y] for i in range(3)]
        sol_ref[y] = start_ref[y] + combine(gain, g[:2])
        res_ref[y] = combine(poly, g)
    for c in sends:
        c.wait_send()


def hand_over(a_ref, b_ref, sol_ref, res_ref):
    sol_ref[...] = a_ref[...]
    res_ref[...] = b_ref[...]


def local(sizes, links, eigvecs, eig_real, eig_imag, rhs):
    nt, nz, nx = sizes
    plane = nz * nx
    ny, dof, lanes = rhs.shape[3:]
    half = lanes // 2
    field = (ny, dof, lanes)
    ndir = links.shape[4]
    slots = sum(1 if n == 2 else 2 for n in sizes)
    far = 1 if nt == 2 else 2
    part = half // plane
    rounds = SWEEPS + 1
    everyone = nt * plane
    direct = everyone if everyone <= DIRECT else 1
    width = sum(pad_to(n * dof, 128) for n in (3, slots - far, far))
    vmem, dma = pltpu.VMEM, pltpu.SemaphoreType.DMA
    spec = pl.BlockSpec(memory_space=pltpu.VMEM)
    sol, res = pl.pallas_call(
        functools.partial(kernel, sizes, field),
        out_shape=[jax.ShapeDtypeStruct(field, F32)] * 2,
        in_specs=[pl.BlockSpec(memory_space=pl.ANY)] * 5,
        out_specs=[spec] * 2,
        scratch_shapes=[
            vmem((ndir, ny, links.shape[5]), F32),
            vmem(field, F32),
            vmem(field, F32),
            vmem((1, half), F32),
            vmem((1, half), F32),
            vmem((ndir * ny * dof, 128), F32),
            vmem((ny, 4 * dof, width), BF16),
            vmem((ny, 2 * dof, lanes), F32),
            vmem((ny, dof, 2 * lanes), BF16),
            vmem((rounds,) + field, F32),
            vmem((rounds, slots) + field, F32),
            vmem((ny, 4 * dof, lanes), BF16),
            vmem(field, F32),
            vmem((3,) + field, F32),
            vmem((plane, part, lanes), F32),
            vmem((plane, part, lanes), F32),
            vmem((nt, part, lanes), F32),
            vmem((plane, part, lanes), F32),
            vmem((2, half, lanes), F32),
            vmem((2, nt, 4, lanes), F32),
            vmem((2, plane, 4, lanes), F32),
            vmem((direct, 4, lanes), F32),
            dma((5,)),
            dma((rounds, slots, ny)),
            dma((rounds, slots, ny)),
            dma((plane,)),
            dma((plane,)),
            dma((nt,)),
            dma((nt,)),
            dma((plane,)),
            dma((plane,)),
            dma((2, nt)),
            dma((2, nt)),
            dma((2, plane)),
            dma((2, plane)),
            dma((direct,)),
            dma((direct,)),
        ],
        compiler_params=pltpu.CompilerParams(collective_id=0, has_side_effects=True),
    )(
        links.reshape(links.shape[3:]).transpose(1, 0, 2),
        eigvecs.reshape(field),
        eig_real.reshape(1, -1),
        eig_imag.reshape(1, -1),
        rhs.reshape(field),
    )
    sol, res = pl.pallas_call(
        hand_over,
        out_shape=[jax.ShapeDtypeStruct(field, F32)] * 2,
        in_specs=[spec] * 2,
        out_specs=[spec] * 2,
    )(sol, res)
    return (sol.reshape(rhs.shape), res.reshape(rhs.shape))


def solution(mesh):
    whole = P("ta", "gz", "xy", None, None, None)
    sizes = tuple(mesh.shape[a] for a in ("ta", "gz", "xy"))
    return jax.shard_map(
        functools.partial(local, sizes),
        mesh=mesh,
        in_specs=(whole, whole, P(), P(), whole),
        out_specs=(whole, whole),
        check_vma=False,
    )
```

time: 57.5 us -> 49.9 us (0.87)
  Pallas kernels: 56.6 us -> 49.1 us
    pallas_call x1, Pallas kernels: 55 us -> 47.5 us  [local(): pl.pallas_call(functools.partial(kernel, sizes, field), out_shape=[jax.Sh...]
where the time goes in v1:
time: 49.9 us; the launch traced here: 49.8 us
  Pallas kernels  49.1 us (98%)
  between operations  0.64 us (1%)
    pallas_call x1, Pallas kernels, local(): pl.pallas_call(functools.partial(kernel, sizes, field), out_shape=[jax.Sh...  47.5 us
    pallas_call x1, Pallas kernels, local(): pl.pallas_call(hand_over, out_shape=[jax.ShapeDtypeStruct(field, F32)] *...  1.62 us

profile of v1, /device:TPU:0, one launch (start us, length us, event | category | flops | bytes accessed | tf_op | source)
XLA Modules:
  0.0 49.8 jit_solution(2666774223514337064)
XLA Ops:
  0.6 47.5 %shard_map.68 = (f32[4,48,128]{2,1,0:T(8,128)}, f32[4,48,128]{2,1,0:T(8,128)}) custom-call(f32[9,4,4608]{2,1,0:T(4,128)} %bitcast.9, f32[4,48,128]{2,1,0:T(8,128)} %bitcast.10, f32[1,64]{1,0:T(1,128)} %bitcast.12, f32[1,64]{1,0:T(1,128)} %bitcast.13, f32[4,48,128]{2,1,0:T(8,128)} %bitcast.11), custom_call_target="tpu_custom_call" | custom-call | tf_op jit(solution)/shard_map/pallas_call | solution.py:475
  48.1 1.6 %shard_map.69 = (f32[4,48,128]{2,1,0:T(8,128)}, f32[4,48,128]{2,1,0:T(8,128)}) custom-call(f32[4,48,128]{2,1,0:T(8,128)} %get-tuple-element.6.a_ref, f32[4,48,128]{2,1,0:T(8,128)} %get-tuple-element.7.b_ref), custom_call_target="tpu_custom_call" | custom-call | tf_op jit(solution)/shard_map/pallas_call | solution.py:527

commit v2 on v1

--- a/solution.py
+++ b/solution.py
@@ -8,6 +8,8 @@
 from jax.sharding import PartitionSpec as P
 
 SWEEPS = 4
+LEAD = 0
+AHEAD = 0
 DIRECT = 32
 MESH = pl.DeviceIdType.MESH
 F32, BF16 = jnp.float32, jnp.bfloat16
@@ -28,7 +30,7 @@
 
 def kernel(
     sizes, dims, links_hbm, v_hbm, er_hbm, ei_hbm, rhs_hbm, sol_ref, res_ref,
-    links, v_ref, rhs_ref, er_ref, ei_ref, flat, mats, acc, pcs, fields, halos, vw, start_ref,
+    links, v_ref, rhs_ref, er_ref, ei_ref, flat, mats, acc, pcs, fields, halos, vw, image_ref, start_ref,
     g_ref, cpart, rs_buf, ct_buf, ag_buf, ec, st_buf, sp_buf, sd_buf,
     in_sem, halo_send, halo_recv, rs_send, rs_recv, ct_send, ct_recv, ag_send, ag_recv,
     st_send, st_recv, sp_send, sp_recv, sd_send, sd_recv,
@@ -49,9 +51,19 @@
         c.start()
         loads.append(c)
 
+    def ranked(*ns):
+        steps = [()]
+        for n in ns:
+            steps = [o + (d,) for o in steps for d in range(n)]
+        steps.sort(key=lambda o: -sum(min(d, n - d) for d, n in zip(o, ns)))
+        return steps[-1:] + steps[:-1]
+
+    plane_steps, all_steps = ranked(nz, nx), ranked(nt, nz, nx)
+
     def plane_peer(k):
-        p = lax.rem(me + k, plane)
-        return p, {"ta": it, "gz": lax.div(p, nx), "xy": lax.rem(p, nx)}
+        dz, dx = plane_steps[k]
+        z, x = lax.rem(iz + dz, nz), lax.rem(ix + dx, nx)
+        return z * nx + x, {"ta": it, "gz": z, "xy": x}
 
     def time_peer(k):
         p = lax.rem(it + k, nt)
@@ -61,9 +73,9 @@
     rank = it * plane + me
 
     def any_peer(k):
-        p = lax.rem(rank + k, everyone)
-        r = lax.rem(p, plane)
-        return p, {"ta": lax.div(p, plane), "gz": lax.div(r, nx), "xy": lax.rem(r, nx)}
+        dt, dz, dx = all_steps[k]
+        t, z, x = lax.rem(it + dt, nt), lax.rem(iz + dz, nz), lax.rem(ix + dx, nx)
+        return t * plane + z * nx + x, {"ta": t, "gz": z, "xy": x}
 
     direct = everyone <= DIRECT
     greeted = [plane_peer(k)[1] for k in range(1, plane)]
@@ -168,6 +180,9 @@
     one = jnp.where(low, 1.0, 0.0).astype(F32)
 
     loads[0].wait()
+    pl.semaphore_wait(barrier, len(greeted))
+    for y in range(ny):
+        send_chunk(0, v_ref, y, ("ta",))
     loads[1].wait()
     rows = pair(v_ref[...].reshape(ny * dof, lanes))
     cross = lax.dot_general(
@@ -178,7 +193,6 @@
     corr = cross[:half] - jsign * swap(cross[half:])
     for p in range(plane):
         cpart[p] = corr[p * part : (p + 1) * part]
-    pl.semaphore_wait(barrier, len(greeted))
     rs_copies = []
     for k in range(1, plane):
         p, target = plane_peer(k)
@@ -193,6 +207,8 @@
     sends += rs_copies
     for y in range(ny):
         send_chunk(0, v_ref, y, ("xy", "gz"))
+    for y in range(AHEAD):
+        send_chunk(1, rhs_ref, y)
 
     loads[3].wait()
     loads[4].wait()
@@ -305,8 +321,8 @@
     recv_all(rs_copies)
     ct_buf[it] = add_slots(rs_buf, plane)
     ct_copies = share(ct_buf, it, nt, time_peer, ct_send, ct_recv)
-    for y in range(ny):
-        send_chunk(0, v_ref, y, ("ta",))
+    for y in range(AHEAD, ny):
+        send_chunk(1, rhs_ref, y)
 
     for y in range(ny):
         build(y)
@@ -314,6 +330,9 @@
         pcs[y] = pair(v_ref[y])
     begin()
 
+    inverse = 1.0 / theta
+    for y in range(ny):
+        middle(0, y)
     recv_all(ct_copies)
     total = add_slots(ct_buf, nt)
     mine = pl.ds(me * part, part)
@@ -321,29 +340,42 @@
     ag_copies = share(ag_buf, me, plane, plane_peer, ag_send, ag_recv)
 
     for y in range(ny):
-        middle(0, y)
-    inverse = 1.0 / theta
-    for y in range(ny):
         v = v_ref[y]
         w = (v - finish(0, y)) * inverse
+        image_ref[y] = w
+        send_chunk(2, image_ref, y)
         for i, piece in enumerate(split(w) + split(v)):
             vw[y, i * dof : (i + 1) * dof] = piece
+    for y in range(ny):
+        pcs[y] = pair(rhs_ref[y])
+    begin()
+    for y in range(ny):
+        middle(1, y)
+
+    for y in range(ny):
+        fields[1, y] = finish(1, y)
+    for y in range(ny):
+        pcs[y] = pair(image_ref[y])
+    begin()
+    for y in range(ny):
+        middle(2, y)
 
     recv_all(ag_copies)
     coef = jnp.concatenate([ag_buf[p] for p in range(plane)], 0)
     block = pair(jnp.concatenate([coef, jsign * swap(coef)], 0))
 
-    def expand(y, i):
-        out = jnp.dot(vw[y, i * dof : (i + 2) * dof], block, preferred_element_type=F32)
+    def expand(left):
+        out = jnp.dot(left, block, preferred_element_type=F32)
         return out[:dof, :lanes] + (out[:dof, lanes:] + out[dof:, :lanes])
 
     for y in range(ny):
-        r = rhs_ref[y] - expand(y, 0)
-        fields[0, y] = r
-        send_chunk(1, fields.at[0], y)
+        r = fields[1, y] - expand(jnp.concatenate(split(finish(2, y)), 0))
+        fields[1, y] = r
+        send_chunk(3, fields.at[1], y)
         pcs[y] = pair(r)
     for y in range(ny):
-        start_ref[y] = expand(y, 2)
+        fields[0, y] = rhs_ref[y] - expand(vw[y, :two])
+        start_ref[y] = expand(vw[y, two:])
 
     def fold(x):
         return jnp.sum(x.reshape(dof // 8, 8, lanes), axis=0)
@@ -395,22 +427,22 @@
 
     def step(rnd, y):
         out = finish(rnd, y)
-        fields[rnd, y] = out
-        if rnd < SWEEPS:
-            send_chunk(rnd + 1, fields.at[rnd], y)
+        fields[rnd - 1, y] = out
+        if rnd < rounds - 1:
+            send_chunk(rnd + 1, fields.at[rnd - 1], y)
             pcs[y] = pair(out)
 
-    LEAD = 2
     poly = gain = None
     sums = None
-    for rnd in range(1, SWEEPS + 1):
+    rounds = SWEEPS + 2
+    for rnd in range(3, rounds):
         begin()
-        if rnd == 3:
+        if rnd == 4:
             for y in range(ny):
                 sums = add(sums, partials(fields[0, y], fields[1, y], fields[2, y]))
             st_buf[0, it] = gram(sums)
             early = share(st_buf.at[0], it, nt, time_peer, st_send.at[0], st_recv.at[0])
-        if rnd == 4:
+        if rnd == 5:
             recv_all(early)
             sp_buf[0, me] = add_slots(st_buf.at[0], nt)
             early = share(sp_buf.at[0], me, plane, plane_peer, sp_send.at[0], sp_recv.at[0])
@@ -466,7 +498,7 @@
     slots = sum(1 if n == 2 else 2 for n in sizes)
     far = 1 if nt == 2 else 2
     part = half // plane
-    rounds = SWEEPS + 1
+    rounds = SWEEPS + 2
     everyone = nt * plane
     direct = everyone if everyone <= DIRECT else 1
     width = sum(pad_to(n * dof, 128) for n in (3, slots - far, far))
@@ -474,7 +506,7 @@
     spec = pl.BlockSpec(memory_space=pltpu.VMEM)
     sol, res = pl.pallas_call(
         functools.partial(kernel, sizes, field),
-        out_shape=[jax.ShapeDtypeStruct(field, F32)] * 2,
+        out_shape=[vmem(field, F32)] * 2,
         in_specs=[pl.BlockSpec(memory_space=pl.ANY)] * 5,
         out_specs=[spec] * 2,
         scratch_shapes=[
@@ -487,9 +519,10 @@
             vmem((ny, 4 * dof, width), BF16),
             vmem((ny, 2 * dof, lanes), F32),
             vmem((ny, dof, 2 * lanes), BF16),
-            vmem((rounds,) + field, F32),
+            vmem((SWEEPS + 1,) + field, F32),
             vmem((rounds, slots) + field, F32),
             vmem((ny, 4 * dof, lanes), BF16),
+            vmem(field, F32),
             vmem(field, F32),
             vmem((3,) + field, F32),
             vmem((plane, part, lanes), F32),
@@ -529,7 +562,7 @@
         out_shape=[jax.ShapeDtypeStruct(field, F32)] * 2,
         in_specs=[spec] * 2,
         out_specs=[spec] * 2,
-    )(sol, res)
+    )(*(pltpu.with_memory_space_constraint(x, pltpu.VMEM) for x in (sol, res)))
     return (sol.reshape(rhs.shape), res.reshape(rhs.shape))
 
 

time: 49.9 us -> 45.5 us (0.912)
  Pallas kernels: 49.1 us -> 44.7 us
    pallas_call x1, Pallas kernels: 47.5 us -> 44 us  [local(): pl.pallas_call(functools.partial(kernel, sizes, field), out_shape=[vmem(f...]
    pallas_call x1, Pallas kernels: 1.62 us -> 0.69 us  [local(): pl.pallas_call(hand_over, out_shape=[jax.ShapeDtypeStruct(field, F32)] *...]
where the time goes in v2:
time: 45.5 us; the launch traced here: 45.4 us
  Pallas kernels  44.7 us (98%)
  between operations  0.64 us (1%)
    pallas_call x1, Pallas kernels, local(): pl.pallas_call(functools.partial(kernel, sizes, field), out_shape=[vmem(f...  44 us

profile of v2, /device:TPU:0, one launch (start us, length us, event | category | flops | bytes accessed | tf_op | source)
XLA Modules:
  0.0 45.4 jit_solution(7499232209336470917)
XLA Ops:
  0.6 44.0 %shard_map.68 = (f32[4,48,128]{2,1,0:T(8,128)S(1)}, f32[4,48,128]{2,1,0:T(8,128)S(1)}) custom-call(f32[9,4,4608]{2,1,0:T(4,128)} %bitcast.9, f32[4,48,128]{2,1,0:T(8,128)} %bitcast.10, f32[1,64]{1,0:T(1,128)} %bitcast.12, f32[1,64]{1,0:T(1,128)} %bitcast.13, f32[4,48,128]{2,1,0:T(8,128)} %bitcast.11), custom_call_target="tpu_custom_call" | custom-call | tf_op jit(solution)/shard_map/pallas_call | solution.py:507
  44.7 0.7 %shard_map.69 = (f32[4,48,128]{2,1,0:T(8,128)}, f32[4,48,128]{2,1,0:T(8,128)}) custom-call(f32[4,48,128]{2,1,0:T(8,128)S(1)} %get-tuple-element.6.a_ref, f32[4,48,128]{2,1,0:T(8,128)S(1)} %get-tuple-element.7.b_ref), custom_call_target="tpu_custom_call" | custom-call | tf_op jit(solution)/shard_map/pallas_call | solution.py:560

commit v3 on v2

--- a/solution.py
+++ b/solution.py
@@ -9,7 +9,8 @@
 
 SWEEPS = 4
 LEAD = 0
-AHEAD = 0
+LAG = 5
+EARLY = 2
 DIRECT = 32
 MESH = pl.DeviceIdType.MESH
 F32, BF16 = jnp.float32, jnp.bfloat16
@@ -43,6 +44,39 @@
     me = iz * nx + ix
     part = half // plane
 
+    def ranked(*ns):
+        steps = [()]
+        for n in ns:
+            steps = [o + (d,) for o in steps for d in range(n)]
+        steps.sort(key=lambda o: -sum(min(d, n - d) for d, n in zip(o, ns)))
+        return steps[-1:] + steps[:-1]
+
+    plane_steps, all_steps = ranked(nz, nx), ranked(nt, nz, nx)
+
+    def plane_peer(k):
+        dz, dx = plane_steps[k]
+        z, x = lax.rem(iz + dz, nz), lax.rem(ix + dx, nx)
+        return z * nx + x, {"ta": it, "gz": z, "xy": x}
+
+    def time_peer(k):
+        p = lax.rem(it + k, nt)
+        return p, {"ta": p, "gz": iz, "xy": ix}
+
+    everyone = nt * plane
+    rank = it * plane + me
+
+    def any_peer(k):
+        dt, dz, dx = all_steps[k]
+        t, z, x = lax.rem(it + dt, nt), lax.rem(iz + dz, nz), lax.rem(ix + dx, nx)
+        return t * plane + z * nx + x, {"ta": t, "gz": z, "xy": x}
+
+    direct = everyone <= DIRECT
+    greeted = [plane_peer(k)[1] for k in range(1, plane)]
+    greeted += [time_peer(k)[1] for k in range(1, nt)]
+    barrier = pltpu.get_barrier_semaphore()
+    for target in greeted:
+        pl.semaphore_signal(barrier, inc=1, device_id=target, device_id_type=MESH)
+
     loads = []
     for i, (src, dst) in enumerate(
         ((v_hbm, v_ref), (rhs_hbm, rhs_ref), (links_hbm, links), (er_hbm, er_ref), (ei_hbm, ei_ref))
@@ -50,39 +84,6 @@
         c = pltpu.make_async_copy(src, dst, in_sem.at[i])
         c.start()
         loads.append(c)
-
-    def ranked(*ns):
-        steps = [()]
-        for n in ns:
-            steps = [o + (d,) for o in steps for d in range(n)]
-        steps.sort(key=lambda o: -sum(min(d, n - d) for d, n in zip(o, ns)))
-        return steps[-1:] + steps[:-1]
-
-    plane_steps, all_steps = ranked(nz, nx), ranked(nt, nz, nx)
-
-    def plane_peer(k):
-        dz, dx = plane_steps[k]
-        z, x = lax.rem(iz + dz, nz), lax.rem(ix + dx, nx)
-        return z * nx + x, {"ta": it, "gz": z, "xy": x}
-
-    def time_peer(k):
-        p = lax.rem(it + k, nt)
-        return p, {"ta": p, "gz": iz, "xy": ix}
-
-    everyone = nt * plane
-    rank = it * plane + me
-
-    def any_peer(k):
-        dt, dz, dx = all_steps[k]
-        t, z, x = lax.rem(it + dt, nt), lax.rem(iz + dz, nz), lax.rem(ix + dx, nx)
-        return t * plane + z * nx + x, {"ta": t, "gz": z, "xy": x}
-
-    direct = everyone <= DIRECT
-    greeted = [plane_peer(k)[1] for k in range(1, plane)]
-    greeted += [time_peer(k)[1] for k in range(1, nt)]
-    barrier = pltpu.get_barrier_semaphore()
-    for target in greeted:
-        pl.semaphore_signal(barrier, inc=1, device_id=target, device_id_type=MESH)
 
     def neighbours(axis, index, n):
         base = {"ta": it, "gz": iz, "xy": ix}
@@ -109,10 +110,8 @@
     far, near = groups["ta"], groups["xy"] + groups["gz"]
     sends = []
 
-    def send_chunk(rnd, src, y, axes=("ta", "xy", "gz")):
-        for axis, s, target in outgoing:
-            if axis not in axes:
-                continue
+    def send_to(rnd, src, y, targets):
+        for axis, s, target in targets:
             c = pltpu.make_async_remote_copy(
                 src_ref=src.at[y], dst_ref=halos.at[rnd, s, y],
                 send_sem=halo_send.at[rnd, s, y], recv_sem=halo_recv.at[rnd, s, y],
@@ -120,6 +119,23 @@
             )
             c.start()
             sends.append(c)
+
+    first_far, second_far = outgoing[:1], outgoing[1 : len(far)]
+    beside = outgoing[len(far) :]
+
+    def send_far(rnd, src, y):
+        send_to(rnd, src, y, first_far)
+        if rnd == LAG:
+            if y:
+                send_to(rnd, src, y - 1, second_far)
+            if y == ny - 1:
+                send_to(rnd, src, y, second_far)
+        else:
+            send_to(rnd, src, y, second_far)
+
+    def send_chunk(rnd, src, y):
+        send_far(rnd, src, y)
+        send_to(rnd, src, y, beside)
 
     def arrived(rnd, s, y):
         pltpu.make_async_remote_copy(
@@ -165,24 +181,13 @@
     def imag(c):
         return jnp.where(low, swap(c), c)
 
-    def factor(c):
-        return real(c), imag(c) * jsign
-
     def times(f, x):
         return f[0] * x + f[1] * swap(x)
 
-    def mul(a, b):
-        return times(factor(a), b)
-
-    def conj(a):
-        return -jsign * a
-
-    one = jnp.where(low, 1.0, 0.0).astype(F32)
-
     loads[0].wait()
     pl.semaphore_wait(barrier, len(greeted))
     for y in range(ny):
-        send_chunk(0, v_ref, y, ("ta",))
+        send_far(0, v_ref, y)
     loads[1].wait()
     rows = pair(v_ref[...].reshape(ny * dof, lanes))
     cross = lax.dot_general(
@@ -206,9 +211,7 @@
     rs_buf[me] = cpart[me]
     sends += rs_copies
     for y in range(ny):
-        send_chunk(0, v_ref, y, ("xy", "gz"))
-    for y in range(AHEAD):
-        send_chunk(1, rhs_ref, y)
+        send_to(0, v_ref, y, beside)
 
     loads[3].wait()
     loads[4].wait()
@@ -300,9 +303,9 @@
         )
         return out[:two, :lanes] + (out[:two, lanes:] + out[two:, :lanes])
 
-    def begin():
+    def begin(a=0):
         for y in range(ny):
-            acc[y] = product(y, 0, [pcs[y], pcs[(y + 1) % ny], pcs[(y - 1) % ny]])
+            acc[a, y] = product(y, 0, [pcs[y], pcs[(y + 1) % ny], pcs[(y - 1) % ny]])
 
     def halo_blocks(rnd, y, group):
         blocks = []
@@ -311,18 +314,20 @@
             blocks.append(pair(halos[rnd, s, y]))
         return blocks
 
-    def middle(rnd, y):
-        acc[y] += product(y, 1, halo_blocks(rnd, y, near))
-
-    def finish(rnd, y):
-        t = acc[y] + product(y, 2, halo_blocks(rnd, y, far))
+    def middle(rnd, y, a=0):
+        acc[a, y] += product(y, 1, halo_blocks(rnd, y, near))
+
+    def finish(rnd, y, a=0):
+        t = acc[a, y] + product(y, 2, halo_blocks(rnd, y, far))
         return t[:dof] + jsign * swap(t[dof:])
 
     recv_all(rs_copies)
     ct_buf[it] = add_slots(rs_buf, plane)
     ct_copies = share(ct_buf, it, nt, time_peer, ct_send, ct_recv)
-    for y in range(AHEAD, ny):
-        send_chunk(1, rhs_ref, y)
+    for y in range(EARLY):
+        send_far(1, rhs_ref, y)
+    for y in range(ny):
+        send_to(1, rhs_ref, y, beside)
 
     for y in range(ny):
         build(y)
@@ -333,19 +338,22 @@
     inverse = 1.0 / theta
     for y in range(ny):
         middle(0, y)
+    for y in range(ny):
+        v = v_ref[y]
+        w = (v - finish(0, y)) * inverse
+        image_ref[y] = w
+        send_far(2, image_ref, y)
+        if y + EARLY < ny:
+            send_far(1, rhs_ref, y + EARLY)
+        for i, piece in enumerate(split(w) + split(v)):
+            vw[y, i * dof : (i + 1) * dof] = piece
     recv_all(ct_copies)
     total = add_slots(ct_buf, nt)
     mine = pl.ds(me * part, part)
     ag_buf[me] = total * ec[0, mine] + swap(total) * ec[1, mine]
     ag_copies = share(ag_buf, me, plane, plane_peer, ag_send, ag_recv)
-
-    for y in range(ny):
-        v = v_ref[y]
-        w = (v - finish(0, y)) * inverse
-        image_ref[y] = w
-        send_chunk(2, image_ref, y)
-        for i, piece in enumerate(split(w) + split(v)):
-            vw[y, i * dof : (i + 1) * dof] = piece
+    for y in range(ny):
+        send_to(2, image_ref, y, beside)
     for y in range(ny):
         pcs[y] = pair(rhs_ref[y])
     begin()
@@ -353,12 +361,10 @@
         middle(1, y)
 
     for y in range(ny):
-        fields[1, y] = finish(1, y)
-    for y in range(ny):
         pcs[y] = pair(image_ref[y])
-    begin()
-    for y in range(ny):
-        middle(2, y)
+    begin(1)
+    for y in range(ny):
+        middle(2, y, 1)
 
     recv_all(ag_copies)
     coef = jnp.concatenate([ag_buf[p] for p in range(plane)], 0)
@@ -369,7 +375,7 @@
         return out[:dof, :lanes] + (out[:dof, lanes:] + out[dof:, :lanes])
 
     for y in range(ny):
-        r = fields[1, y] - expand(jnp.concatenate(split(finish(2, y)), 0))
+        r = finish(1, y) - expand(jnp.concatenate(split(finish(2, y, 1)), 0))
         fields[1, y] = r
         send_chunk(3, fields.at[1], y)
         pcs[y] = pair(r)
@@ -385,38 +391,44 @@
         s0, t0 = swap(x0), swap(u0)
         return [
             fold(p)
-            for p in (u0 * x0, u0 * s0, u1 * x0, u1 * s0, u1 * u0, u1 * t0, u0 * u0, u1 * u1)
+            for p in (u0 * x0, u1 * x0, u1 * u0, u0 * u0, u0 * s0, u1 * s0, u1 * t0, u1 * u1)
         ]
 
     def add(a, b):
         return b if a is None else [p + q for p, q in zip(a, b)]
 
     def gram(sums):
-        s = [jnp.sum(p, axis=0, keepdims=True) for p in sums]
-        out = [
-            jnp.where(low, s[i] + swap(s[i]), swap(s[i + 1]) - s[i + 1]) for i in (0, 2, 4)
-        ]
-        out.append(jnp.where(low, s[6] + swap(s[6]), s[7] + swap(s[7])))
-        row = lax.broadcasted_iota(jnp.int32, (4, lanes), 0)
-        x = out[3]
-        for i in (2, 1, 0):
-            x = jnp.where(row == i, out[i], x)
-        return x
+        row = lax.broadcasted_iota(jnp.int32, (8, lanes), 0)
+        x = jnp.sum(sums[7], axis=0, keepdims=True)
+        for i in range(7):
+            x = jnp.where(row == i, jnp.sum(sums[i], axis=0, keepdims=True), x)
+        r = swap(x)
+        y = r + jnp.where((row < 4) | (row == 7), x, -x)
+        return jnp.where(low, y[:4], y[4:])
+
+    def product_of(x, y):
+        return x[0] * y[0] - x[1] * y[1], x[0] * y[1] + x[1] * y[0]
+
+    def inner(x, y):
+        return x[0] * y[0] + x[1] * y[1], x[0] * y[1] - x[1] * y[0]
 
     def steps(total):
-        a, b, c, d = (total[i : i + 1] for i in range(4))
-        b0 = a / real(d)
-        e = mul(conj(b0), c)
-        num = mul(conj(b0), b) - mul(real(mul(conj(b0), b0)) * one, c)
-        near_one = one - b0
-        size0 = real(mul(conj(near_one), near_one))
-        size1 = real(mul(conj(b0), b0))
-        den = size0 * real(d) + size1 * imag(d) + 2.0 * real(mul(near_one, e))
-        b1 = num / den
-        both = mul(b0, b1)
-        mixed = b0 + b1 - both
-        poly = [factor(x) for x in (one - mixed, mixed - both, both)]
-        gain = [factor(theta * x) for x in (mixed, both)]
+        r, i = real(total), imag(total)
+        a, b, c = ((r[k : k + 1], i[k : k + 1]) for k in range(3))
+        size, other = r[3:4], i[3:4]
+        b0 = (a[0] / size, a[1] / size)
+        power = b0[0] * b0[0] + b0[1] * b0[1]
+        num = inner(b0, b)
+        num = (num[0] - power * c[0], num[1] - power * c[1])
+        left = (1.0 - b0[0], -b0[1])
+        e = product_of(left, inner(b0, c))
+        den = (left[0] * left[0] + left[1] * left[1]) * size + power * other + 2.0 * e[0]
+        b1 = (num[0] / den, num[1] / den)
+        both = product_of(b0, b1)
+        mixed = tuple(p + q - t for p, q, t in zip(b0, b1, both))
+        poly = ((1.0 - mixed[0], -mixed[1]), tuple(p - q for p, q in zip(mixed, both)), both)
+        poly = [(p, q * jsign) for p, q in poly]
+        gain = [(theta * p, theta * q * jsign) for p, q in (mixed, both)]
         return poly, gain
 
     def combine(poly, xs):
@@ -458,12 +470,18 @@
         f = [fields[i, y] for i in range(SWEEPS + 1)]
         g = [combine(poly, f[i : i + 3]) for i in range(3)]
         for i in range(3):
-            g_ref[i, y] = g[i]
+            g_ref[2 * i, y] = g[i]
+            g_ref[2 * i + 1, y] = swap(g[i])
         start_ref[y] = start_ref[y] + combine(gain, f[:2])
         sums = add(sums, partials(*g))
+    def drain():
+        for c in sends:
+            c.wait_send()
+
     if direct:
         sd_buf[rank] = gram(sums)
         last = share(sd_buf, rank, everyone, any_peer, sd_send, sd_recv)
+        drain()
         recv_all(last)
         total = add_slots(sd_buf, everyone)
     else:
@@ -472,15 +490,19 @@
         recv_all(last)
         sp_buf[1, me] = add_slots(st_buf.at[1], nt)
         last = share(sp_buf.at[1], me, plane, plane_peer, sp_send.at[1], sp_recv.at[1])
+        drain()
         recv_all(last)
         total = add_slots(sp_buf.at[1], plane)
     poly, gain = steps(total)
-    for y in range(ny):
-        g = [g_ref[i, y] for i in range(3)]
-        sol_ref[y] = start_ref[y] + combine(gain, g[:2])
-        res_ref[y] = combine(poly, g)
-    for c in sends:
-        c.wait_send()
+    def blend(f, y):
+        out = f[0][0] * g_ref[0, y] + f[0][1] * g_ref[1, y]
+        for i in range(1, len(f)):
+            out = out + (f[i][0] * g_ref[2 * i, y] + f[i][1] * g_ref[2 * i + 1, y])
+        return out
+
+    for y in range(ny):
+        sol_ref[y] = start_ref[y] + blend(gain, y)
+        res_ref[y] = blend(poly, y)
 
 
 def hand_over(a_ref, b_ref, sol_ref, res_ref):
@@ -517,14 +539,14 @@
             vmem((1, half), F32),
             vmem((ndir * ny * dof, 128), F32),
             vmem((ny, 4 * dof, width), BF16),
-            vmem((ny, 2 * dof, lanes), F32),
+            vmem((2, ny, 2 * dof, lanes), F32),
             vmem((ny, dof, 2 * lanes), BF16),
             vmem((SWEEPS + 1,) + field, F32),
             vmem((rounds, slots) + field, F32),
             vmem((ny, 4 * dof, lanes), BF16),
             vmem(field, F32),
             vmem(field, F32),
-            vmem((3,) + field, F32),
+            vmem((6,) + field, F32),
             vmem((plane, part, lanes), F32),
             vmem((plane, part, lanes), F32),
             vmem((nt, part, lanes), F32),

time: 45.5 us -> 44.2 us (0.971)
  Pallas kernels: 44.7 us -> 43.5 us
    pallas_call x1, Pallas kernels: 44 us -> 42.8 us  [local(): pl.pallas_call(functools.partial(kernel, sizes, field), out_shape=[vmem(f...]
where the time goes in v3:
time: 44.2 us; the launch traced here: 44.1 us
  Pallas kernels  43.5 us (98%)
  between operations  0.64 us (1%)
    pallas_call x1, Pallas kernels, local(): pl.pallas_call(functools.partial(kernel, sizes, field), out_shape=[vmem(f...  42.8 us

profile of v3, /device:TPU:0, one launch (start us, length us, event | category | flops | bytes accessed | tf_op | source)
XLA Modules:
  0.0 44.1 jit_solution(17846597105247298855)
XLA Ops:
  0.6 42.8 %shard_map.68 = (f32[4,48,128]{2,1,0:T(8,128)S(1)}, f32[4,48,128]{2,1,0:T(8,128)S(1)}) custom-call(f32[9,4,4608]{2,1,0:T(4,128)} %bitcast.9, f32[4,48,128]{2,1,0:T(8,128)} %bitcast.10, f32[1,64]{1,0:T(1,128)} %bitcast.12, f32[1,64]{1,0:T(1,128)} %bitcast.13, f32[4,48,128]{2,1,0:T(8,128)} %bitcast.11), custom_call_target="tpu_custom_call" | custom-call | tf_op jit(solution)/shard_map/pallas_call | solution.py:529
  43.4 0.7 %shard_map.69 = (f32[4,48,128]{2,1,0:T(8,128)}, f32[4,48,128]{2,1,0:T(8,128)}) custom-call(f32[4,48,128]{2,1,0:T(8,128)S(1)} %get-tuple-element.6.a_ref, f32[4,48,128]{2,1,0:T(8,128)S(1)} %get-tuple-element.7.b_ref), custom_call_target="tpu_custom_call" | custom-call | tf_op jit(solution)/shard_map/pallas_call | solution.py:582

commit v4 on v3

--- a/solution.py
+++ b/solution.py
@@ -33,7 +33,7 @@
     sizes, dims, links_hbm, v_hbm, er_hbm, ei_hbm, rhs_hbm, sol_ref, res_ref,
     links, v_ref, rhs_ref, er_ref, ei_ref, flat, mats, acc, pcs, fields, halos, vw, image_ref, start_ref,
     g_ref, cpart, rs_buf, ct_buf, ag_buf, ec, st_buf, sp_buf, sd_buf,
-    in_sem, halo_send, halo_recv, rs_send, rs_recv, ct_send, ct_recv, ag_send, ag_recv,
+    token, in_sem, halo_send, halo_recv, rs_send, rs_recv, ct_send, ct_recv, ag_send, ag_recv,
     st_send, st_recv, sp_send, sp_recv, sd_send, sd_recv,
 ):
     nt, nz, nx = sizes
@@ -51,7 +51,7 @@
         steps.sort(key=lambda o: -sum(min(d, n - d) for d, n in zip(o, ns)))
         return steps[-1:] + steps[:-1]
 
-    plane_steps, all_steps = ranked(nz, nx), ranked(nt, nz, nx)
+    plane_steps = ranked(nz, nx)
 
     def plane_peer(k):
         dz, dx = plane_steps[k]
@@ -65,17 +65,33 @@
     everyone = nt * plane
     rank = it * plane + me
 
-    def any_peer(k):
-        dt, dz, dx = all_steps[k]
-        t, z, x = lax.rem(it + dt, nt), lax.rem(iz + dz, nz), lax.rem(ix + dx, nx)
-        return t * plane + z * nx + x, {"ta": t, "gz": z, "xy": x}
+    def other(j):
+        p = j + jnp.where(rank <= j, 1, 0)
+        r = lax.rem(p, plane)
+        return p, {"ta": lax.div(p, plane), "gz": lax.div(r, nx), "xy": lax.rem(r, nx)}
 
     direct = everyone <= DIRECT
-    greeted = [plane_peer(k)[1] for k in range(1, plane)]
-    greeted += [time_peer(k)[1] for k in range(1, nt)]
     barrier = pltpu.get_barrier_semaphore()
-    for target in greeted:
-        pl.semaphore_signal(barrier, inc=1, device_id=target, device_id_type=MESH)
+
+    def at_time(p):
+        return {"ta": p, "gz": iz, "xy": ix}
+
+    def signal_when(test, sem, p):
+        @pl.when(test)
+        def _():
+            pl.semaphore_signal(sem, inc=1, device_id=at_time(p), device_id_type=MESH)
+
+    def wait_when(test, sem):
+        @pl.when(test)
+        def _():
+            pl.semaphore_wait(sem, 1)
+
+    above, below = it < nt - 1, it > 0
+    signal_when(above, barrier, it + 1)
+    signal_when(below, barrier, it - 1)
+    for k in range(1, plane):
+        pl.semaphore_signal(barrier, inc=1, device_id=plane_peer(k)[1], device_id_type=MESH)
+    greetings = plane - 1 + jnp.where(above, 1, 0) + jnp.where(below, 1, 0)
 
     loads = []
     for i, (src, dst) in enumerate(
@@ -110,15 +126,19 @@
     far, near = groups["ta"], groups["xy"] + groups["gz"]
     sends = []
 
-    def send_to(rnd, src, y, targets):
+    def send_to(rnd, src, y, targets, start=True):
+        out = []
         for axis, s, target in targets:
             c = pltpu.make_async_remote_copy(
                 src_ref=src.at[y], dst_ref=halos.at[rnd, s, y],
                 send_sem=halo_send.at[rnd, s, y], recv_sem=halo_recv.at[rnd, s, y],
                 device_id=target, device_id_type=MESH,
             )
-            c.start()
-            sends.append(c)
+            if start:
+                c.start()
+            out.append(c)
+        sends.extend(out)
+        return out
 
     first_far, second_far = outgoing[:1], outgoing[1 : len(far)]
     beside = outgoing[len(far) :]
@@ -184,10 +204,24 @@
     def times(f, x):
         return f[0] * x + f[1] * swap(x)
 
+    inner = above & below
+
+    def start_when(test, copies):
+        @pl.when(test)
+        def _():
+            for c in copies:
+                c.start()
+
     loads[0].wait()
-    pl.semaphore_wait(barrier, len(greeted))
-    for y in range(ny):
-        send_far(0, v_ref, y)
+    pl.semaphore_wait(barrier, greetings)
+    if nt > 2:
+        signal_when(it == nt - 2, token.at[0], it - 1)
+        signal_when(it == 1, token.at[1], it + 1)
+    wrapped = []
+    for y in range(ny):
+        send_to(0, v_ref, y, second_far)
+        wrapped += send_to(0, v_ref, y, first_far, False)
+    start_when(inner, wrapped)
     loads[1].wait()
     rows = pair(v_ref[...].reshape(ny * dof, lanes))
     cross = lax.dot_general(
@@ -210,6 +244,12 @@
         rs_copies.append(c)
     rs_buf[me] = cpart[me]
     sends += rs_copies
+    if nt > 2:
+        wait_when(it < nt - 2, token.at[0])
+        signal_when((it < nt - 2) & below, token.at[0], it - 1)
+        wait_when(it > 1, token.at[1])
+        signal_when((it > 1) & above, token.at[1], it + 1)
+    start_when(jnp.logical_not(inner), wrapped)
     for y in range(ny):
         send_to(0, v_ref, y, beside)
 
@@ -480,9 +520,22 @@
 
     if direct:
         sd_buf[rank] = gram(sums)
-        last = share(sd_buf, rank, everyone, any_peer, sd_send, sd_recv)
+        for j in range(everyone - 1):
+            c = pltpu.make_async_remote_copy(
+                src_ref=sd_buf.at[rank], dst_ref=sd_buf.at[rank],
+                send_sem=sd_send.at[j], recv_sem=sd_recv.at[rank],
+                device_id=other(j)[1], device_id_type=MESH,
+            )
+            c.start()
+            sends.append(c)
         drain()
-        recv_all(last)
+        for j in range(everyone - 1):
+            p, target = other(j)
+            pltpu.make_async_remote_copy(
+                src_ref=sd_buf.at[p], dst_ref=sd_buf.at[p],
+                send_sem=sd_send.at[j], recv_sem=sd_recv.at[p],
+                device_id=target, device_id_type=MESH,
+            ).wait_recv()
         total = add_slots(sd_buf, everyone)
     else:
         st_buf[1, it] = gram(sums)
@@ -555,6 +608,7 @@
             vmem((2, nt, 4, lanes), F32),
             vmem((2, plane, 4, lanes), F32),
             vmem((direct, 4, lanes), F32),
+            pltpu.SemaphoreType.REGULAR((2,)),
             dma((5,)),
             dma((rounds, slots, ny)),
             dma((rounds, slots, ny)),

time: 44.2 us -> 43.8 us (level)
  Pallas kernels: 43.5 us -> 43 us
where the time goes in v4:
time: 43.8 us; the launch traced here: 43.7 us
  Pallas kernels  43 us (98%)
  between operations  0.64 us (1%)
    pallas_call x1, Pallas kernels, local(): pl.pallas_call(functools.partial(kernel, sizes, field), out_shape=[vmem(f...  42.3 us

profile of v4, /device:TPU:0, one launch (start us, length us, event | category | flops | bytes accessed | tf_op | source)
XLA Modules:
  0.0 43.7 jit_solution(1409989802776767410)
XLA Ops:
  0.6 42.3 %shard_map.68 = (f32[4,48,128]{2,1,0:T(8,128)S(1)}, f32[4,48,128]{2,1,0:T(8,128)S(1)}) custom-call(f32[9,4,4608]{2,1,0:T(4,128)} %bitcast.9, f32[4,48,128]{2,1,0:T(8,128)} %bitcast.10, f32[1,64]{1,0:T(1,128)} %bitcast.12, f32[1,64]{1,0:T(1,128)} %bitcast.13, f32[4,48,128]{2,1,0:T(8,128)} %bitcast.11), custom_call_target="tpu_custom_call" | custom-call | tf_op jit(solution)/shard_map/pallas_call | solution.py:582
  43.0 0.7 %shard_map.69 = (f32[4,48,128]{2,1,0:T(8,128)}, f32[4,48,128]{2,1,0:T(8,128)}) custom-call(f32[4,48,128]{2,1,0:T(8,128)S(1)} %get-tuple-element.6.a_ref, f32[4,48,128]{2,1,0:T(8,128)S(1)} %get-tuple-element.7.b_ref), custom_call_target="tpu_custom_call" | custom-call | tf_op jit(solution)/shard_map/pallas_call | solution.py:636

commit v5 on v4

--- a/solution.py
+++ b/solution.py
@@ -10,7 +10,7 @@
 SWEEPS = 4
 LEAD = 0
 LAG = 5
-EARLY = 2
+EARLY = 4
 DIRECT = 32
 MESH = pl.DeviceIdType.MESH
 F32, BF16 = jnp.float32, jnp.bfloat16
@@ -213,15 +213,6 @@
                 c.start()
 
     loads[0].wait()
-    pl.semaphore_wait(barrier, greetings)
-    if nt > 2:
-        signal_when(it == nt - 2, token.at[0], it - 1)
-        signal_when(it == 1, token.at[1], it + 1)
-    wrapped = []
-    for y in range(ny):
-        send_to(0, v_ref, y, second_far)
-        wrapped += send_to(0, v_ref, y, first_far, False)
-    start_when(inner, wrapped)
     loads[1].wait()
     rows = pair(v_ref[...].reshape(ny * dof, lanes))
     cross = lax.dot_general(
@@ -232,6 +223,15 @@
     corr = cross[:half] - jsign * swap(cross[half:])
     for p in range(plane):
         cpart[p] = corr[p * part : (p + 1) * part]
+    pl.semaphore_wait(barrier, greetings)
+    if nt > 2:
+        signal_when(it == nt - 2, token.at[0], it - 1)
+        signal_when(it == 1, token.at[1], it + 1)
+    wrapped = []
+    for y in range(ny):
+        send_to(0, v_ref, y, second_far)
+        wrapped += send_to(0, v_ref, y, first_far, False)
+    start_when(inner, wrapped)
     rs_copies = []
     for k in range(1, plane):
         p, target = plane_peer(k)

time: 43.8 us -> 43.9 us (level)
  no operation moved by 1% of the time
where the time goes in v5:
time: 43.9 us; the launch traced here: 43.7 us
  Pallas kernels  43.1 us (98%)
  between operations  0.64 us (1%)
    pallas_call x1, Pallas kernels, local(): pl.pallas_call(functools.partial(kernel, sizes, field), out_shape=[vmem(f...  42.4 us

profile of v5, /device:TPU:0, one launch (start us, length us, event | category | flops | bytes accessed | tf_op | source)
XLA Modules:
  0.0 43.7 jit_solution(2698791084058606352)
XLA Ops:
  0.6 42.4 %shard_map.68 = (f32[4,48,128]{2,1,0:T(8,128)S(1)}, f32[4,48,128]{2,1,0:T(8,128)S(1)}) custom-call(f32[9,4,4608]{2,1,0:T(4,128)} %bitcast.9, f32[4,48,128]{2,1,0:T(8,128)} %bitcast.10, f32[1,64]{1,0:T(1,128)} %bitcast.12, f32[1,64]{1,0:T(1,128)} %bitcast.13, f32[4,48,128]{2,1,0:T(8,128)} %bitcast.11), custom_call_target="tpu_custom_call" | custom-call | tf_op jit(solution)/shard_map/pallas_call | solution.py:582
  43.0 0.7 %shard_map.69 = (f32[4,48,128]{2,1,0:T(8,128)}, f32[4,48,128]{2,1,0:T(8,128)}) custom-call(f32[4,48,128]{2,1,0:T(8,128)S(1)} %get-tuple-element.6.a_ref, f32[4,48,128]{2,1,0:T(8,128)S(1)} %get-tuple-element.7.b_ref), custom_call_target="tpu_custom_call" | custom-call | tf_op jit(solution)/shard_map/pallas_call | solution.py:636
